TPU v7x, 32 devices: a whole 2x2x4 slice. The times are simulated.
32 devices in a mesh: cls: 4 (over y, x), dom: 8 (over z, core).
Axes of the slice: x: 2, y: 2, z: 4, core: 2. Of those that a mesh axis runs over, the one named last changes fastest.
Arguments:
- particles: bfloat16 [256, 2, 110592], P(('cls', 'dom')), may hold values from -18 to 18
- labels: int32 [256, 1], P(('cls', 'dom')), may hold values from 0 to 7; in each aligned block of 8 rows (0 to 7, 8 to 15, ...) at most 2 rows name the same one
- wedge_index: int32 [256], P(('cls', 'dom')), may hold values from 0 to 11
- wedge_table: float32 [12, 110592], replicated, may hold values from 0.05 to 1
Outputs:
- class_average: float32 [8, 2, 110592], P('cls', None, 'dom')
- weight_total: float32 [8, 110592], P('cls', 'dom')
Inputs may be any that keep to these rules, and one draw needn't show every extreme that they name: `labels`: among the rows of one device no class appears more than 2 times, and on some devices one class appears exactly 2 times; every class appears on some device.
All inputs are finite; a program needn't handle non-finite values.
Results may differ from a plain program's by a relative error of at most 0.0003.
Values may be sent and summed in bfloat16 or wider, within the bound.
No kernel may reach another device: no remote copies, remote signals or barrier semaphores. Data moves between devices by JAX's collectives and lax.ppermute only.
A program may use at most 128 MiB of HBM per device.

v0:
```python
import jax
import jax.numpy as jnp
from jax import lax
from jax.sharding import PartitionSpec as P

CLS_GROUP = 2


def per_device(particles, labels, wedge_index, wedge_table):
    n_cls = lax.axis_size("cls")
    n_dom = lax.axis_size("dom")
    p_dev = particles.shape[0]
    voxels = particles.shape[2]
    shard_len = voxels // n_dom
    wedge_count = wedge_table.shape[0]
    label_flat = labels[:, 0]
    parts_four = particles.reshape(p_dev, 2, n_dom, shard_len)
    dom_pos = lax.axis_index("dom")
    table_shard = lax.dynamic_slice_in_dim(wedge_table, dom_pos * shard_len, shard_len, 1)
    got_data = lax.all_to_all(parts_four, "dom", split_axis=2, concat_axis=0, tiled=True)
    got_data = got_data.reshape(n_dom * p_dev, 2, shard_len)
    group_labels, group_wedges = (
        lax.all_gather(label_flat, "dom", axis=0, tiled=True),
        lax.all_gather(wedge_index, "dom", axis=0, tiled=True),
    )
    pick = (group_wedges[:, None] == jnp.arange(wedge_count, dtype=jnp.int32)[None, :]).astype(
        jnp.float32
    )
    weight = jnp.dot(pick, table_shard, precision=lax.Precision.HIGHEST)
    member = (
        jnp.arange(n_cls * CLS_GROUP, dtype=jnp.int32)[:, None] == group_labels[None, :]
    ).astype(jnp.float32)
    weighted = weight[:, None, :] * got_data
    local_sums = jnp.einsum("kp,pcv->kcv", member, weighted, precision=lax.Precision.HIGHEST)
    local_totals = jnp.dot(member, weight * weight, precision=lax.Precision.HIGHEST)
    local_sums = local_sums.reshape(n_cls, CLS_GROUP, 2, shard_len)
    local_totals = local_totals.reshape(n_cls, CLS_GROUP, shard_len)
    summed, totals = (
        lax.psum_scatter(local_sums, "cls", scatter_dimension=0, tiled=True),
        lax.psum_scatter(local_totals, "cls", scatter_dimension=0, tiled=True),
    )
    weighted_sum = summed[0]
    weight_total = totals[0]
    class_average = weighted_sum / (weight_total[:, None, :] + 1.0)
    return (class_average, weight_total)


def solution(mesh):
    return jax.shard_map(
        per_device,
        mesh=mesh,
        in_specs=(P(("cls", "dom"), None, None), P(("cls", "dom"), None), P(("cls", "dom")), P()),
        out_specs=(P("cls", None, "dom"), P("cls", "dom")),
        check_vma=False,
    )
```

profile of v0, /device:TPU:0, one launch (start us, length us, event | category | flops | bytes accessed | tf_op | source)
XLA Modules:
  0.0 185.2 jit_solution(2166439948641008769)
XLA Ops:
  7.2 0.0 copy-start.3
  7.2 0.0 copy-start
  7.2 0.0 copy-start.1
  7.2 6.2 %copy.23 = bf16[8,1,8,2,13824]{4,3,1,0,2:T(2,128)(2,1)} copy(bf16[8,1,8,2,13824]{4,3,2,1,0:T(2,128)(2,1)} %bitcast.34) | data formatting | bytes 7077888 | tf_op jit(solution)/shard_map/reshape | solution.py:17
  13.4 6.4 %all-to-all-start = ((bf16[8,2,8,13824]{3,1,0,2:T(2,128)(2,1)}), bf16[8,2,8,13824]{3,1,0,2:T(2,128)(2,1)}, u32[]{:S(2)}, u32[]{:S(2)}) async-start(bf16[8,2,8,13824]{3,1,0,2:T(2,128)(2,1)} %bitcast.31), calls=%async_computation | async-start | bytes 7077888 | tf_op jit(solution)/shard_map/all_to_all | solution.py:20
  19.8 0.0 all-reduce.8.cloned.1.call-start
  19.8 0.0 copy-done.3
  19.9 0.6 dynamic-slice
  21.1 0.0 copy-done
  21.1 0.2 dynamic-update-slice.1
  21.4 0.0 copy-done.1
  21.4 0.1 bitcast_dynamic-update-slice_fusion
  21.4 78.5 %all-reduce.4 = (s32[64]{0:T(128)S(1)}, s32[64]{0:T(128)S(1)}) all-reduce(s32[64]{0:T(128)S(1)} %dynamic-update-slice.1, s32[64]{0:T(128)S(1)} %bitcast_dynamic-update-slice_fusion), channel_id=1, replica_groups=mesh['cls'=4,'dom'=8] {'dom'}, use_global_device_ids=true, to_apply=%add.1 | all-reduce | flops 128 | bytes 1024
  100.0 2.7 %fusion.6 = f32[64,13824]{1,0:T(8,128)S(1)} fusion(f32[12,110592]{1,0:T(8,128)} %param.7, s32[]{:T(128)S(6)} %select_n.3, s32[64]{0:T(128)S(1)} %get-tuple-element.2), kind=kOutput, calls=%fused_computation.8 | convolution fusion | flops 127402752 | bytes 4423940 | tf_op jit(solution)/shard_map/dot_general | solution.py:29
  102.7 2.1 %fusion.4 = f32[8,13824]{1,0:T(8,128)} fusion(f32[64,13824]{1,0:T(8,128)S(1)} %fusion.6, s32[64]{0:T(128)S(1)} %get-tuple-element.3), kind=kOutput, calls=%fused_computation.6 | convolution fusion | flops 85819904 | bytes 3981568 | tf_op jit(solution)/shard_map/dot_general | solution.py:35
  104.8 2.0 %reshape.47 = f32[4,2,13824]{2,1,0:T(2,128)} reshape(f32[8,13824]{1,0:T(8,128)} %fusion.4) | data formatting | bytes 884736 | tf_op jit(solution)/shard_map/reshape | solution.py:37
  106.8 0.0 all-to-all-done
  106.8 6.4 %fusion = f32[8,8,2,1,13824]{4,2,1,0,3:T(2,128)S(1)} fusion(bf16[8,2,8,13824]{3,1,0,2:T(2,128)(2,1)} %all-to-all-done, f32[8,8,13824]{2,1,0:T(8,128)S(1)} %bitcast.32), kind=kLoop, calls=%fused_computation.1 | loop fusion | flops 3538944 | bytes 14155776 | tf_op jit(solution)/shard_map/mul | solution.py:33
  113.3 0.0 copy-start.2
  113.3 3.1 %fusion.1 = f32[4,2,2,13824]{3,0,2,1:T(4,128)S(1)} fusion(f32[64,2,13824]{2,1,0:T(2,128)S(1)} %bitcast.33, s32[64]{0:T(128)S(1)} %get-tuple-element.3, s32[4,2]{0,1:T(2,128)S(1)} %multiply_add_fusion), kind=kOutput, calls=%fused_computation.2 | convolution fusion | flops 169869824 | bytes 7962912 | tf_op jit(solution)/shard_map/kp,pcv->kcv/dot_general | solution.py:34
  116.4 1.4 copy.13
  117.7 0.0 all-reduce.8.cloned.1.call-update
  117.8 0.0 copy-done.2
  117.8 0.6 dynamic-slice.2
  118.4 55.4 %all-reduce.8.cloned.1.call-done = (f32[4,2,2,13824]{3,2,1,0:T(2,128)}, f32[4,2,13824]{2,1,0:T(2,128)}) async-done(((f32[4,2,2,13824]{3,2,1,0:T(2,128)}, f32[4,2,13824]{2,1,0:T(2,128)}), (f32[4,2,2,13824]{3,2,1,0:T(2,128)}, f32[4,2,13824]{2,1,0:T(2,128)})) %all-reduce.8.cloned.1.call-update) | async-done | bytes 1327120
  173.8 2.2 %broadcast_add_fusion = (f32[2,13824]{1,0:T(2,128)S(1)}, f32[2,13824]{1,0:T(2,128)}) fusion(f32[4,2,13824]{2,1,0:T(2,128)} %get-tuple-element.5, u32[]{:T(128)} %bitcast.13), kind=kLoop, calls=%fused_computation.13 | loop fusion | flops 27648 | bytes 331780 | tf_op jit(solution)/shard_map/add | solution.py:44
  176.0 2.3 %fusion.8 = f32[2,2,13824]{2,1,0:T(2,128)} fusion(f32[4,2,2,13824]{3,2,1,0:T(2,128)} %get-tuple-element.4, u32[]{:T(128)} %bitcast.13, f32[2,13824]{1,0:T(2,128)S(1)} %get-tuple-element.6), kind=kLoop, calls=%fused_computation.11 | loop fusion | flops 55296 | bytes 552964 | tf_op jit(solution)/shard_map/div | solution.py:44
  (3 shorter events, 0.0 us)
Async XLA Ops:
  7.2 12.7 %copy-start.3 = (u32[32]{0:T(128)S(1)}, u32[32]{0:T(128)}, u32[]{:S(2)}) copy-start(u32[32]{0:T(128)} %constant.19) | copy-start | bytes 388
  7.2 13.9 %copy-start = (s32[8]{0:T(128)S(1)}, s32[8]{0:T(128)}, u32[]{:S(2)}) copy-start(s32[8]{0:T(128)} %param.6) | copy-start | bytes 100
  7.2 14.2 %copy-start.1 = (s32[8,1]{0,1:T(1,128)S(1)}, s32[8,1]{0,1:T(1,128)}, u32[]{:S(2)}) copy-start(s32[8,1]{0,1:T(1,128)} %param.5) | copy-start | bytes 100
  13.4 93.4 %all-to-all-start = ((bf16[8,2,8,13824]{3,1,0,2:T(2,128)(2,1)}), bf16[8,2,8,13824]{3,1,0,2:T(2,128)(2,1)}, u32[]{:S(2)}, u32[]{:S(2)}) async-start(bf16[8,2,8,13824]{3,1,0,2:T(2,128)(2,1)} %bitcast.31), calls=%async_computation | async-start | bytes 7077888 | tf_op jit(solution)/shard_map/all_to_all | solution.py:20
  19.8 154.0 %all-reduce.8.cloned.1.call-start = ((), (), s32[]{:S(2)}) async-start(), calls=%async_computation.1 | async-start | bytes 2654208
  113.3 4.5 %copy-start.2 = (u32[32]{0:T(128)S(1)}, u32[32]{0:T(128)}, u32[]{:S(2)}) copy-start(u32[32]{0:T(128)} %constant.31) | copy-start | bytes 388
Sparse Core Ops, SparseCore 0:
  117.9 55.8 all-reduce.7
where the time goes:
time: 186 us; the launch traced here: 185 us
  blocking collectives  78.5 us (42%)
  waiting for transfers between devices  55.5 us (30%)
  between operations  14.8 us (8%)
  local copies, waits for them, and re-layouts  11.2 us (6%)
  other arithmetic  11 us (6%)
  matrix products  7.9 us (4%)
  starting transfers between devices  6.39 us (3%)
    unnamed x1, blocking collectives  78.5 us
    unnamed x2, waiting for transfers between devices  55.5 us
    mul x1, other arithmetic, per_device(): weighted = weight[:, None, :] * got_data  6.44 us
    all_to_all x1, starting transfers between devices, per_device(): lax.all_to_all(parts_four, 'dom', split_axis=2, concat_axis=0, tiled=True)  6.35 us
    reshape x1, local copies, waits for them, and re-layouts, per_device(): parts_four = particles.reshape(p_dev, 2, n_dom, shard_len)  6.24 us
  transfers between devices with their start and end apart: 2, of which 1 were waited for; matrix products, arithmetic and copies ran while one was open for 5% of the time, Pallas kernels for 0%

commit v1 on v0

v1 whole, which is shorter than its diff:
```python
import functools

import jax
import jax.numpy as jnp
from jax import lax
from jax.experimental import pallas as pl
from jax.experimental.pallas import tpu as pltpu
from jax.sharding import PartitionSpec as P

LANES = 128
SUB = 8
CORES = 2
STEPS = 8
TOP = 32000.0
LEAST = 1e-30
VMEM = pl.BlockSpec(memory_space=pltpu.VMEM)
SMEM = pl.BlockSpec(memory_space=pltpu.SMEM)
PARAMS = pltpu.CompilerParams(vmem_limit_bytes=40 * 1024 * 1024)


def padded(rows):
    return -(-(rows + 2) // SUB) * SUB


def partner(index, offset, count):
    if count & (count - 1) == 0:
        return index ^ offset
    return lax.rem(index + offset, count)


def back(index, offset, count):
    if count & (count - 1) == 0:
        return index ^ offset
    return lax.rem(index + count - offset, count)


def pack(total, counts):
    rows = total.shape[0]
    peak = jnp.maximum(jnp.max(jnp.abs(total), axis=0, keepdims=True), LEAST)
    level = jnp.ceil(jnp.log2(peak) * STEPS)
    inverse = TOP * jnp.exp2(level * (-1.0 / STEPS))
    coded = jnp.round(total * inverse)
    extra = padded(rows) - rows
    place = lax.broadcasted_iota(jnp.int32, (extra, LANES), 0)
    tail = jnp.where(place == 0, level, jnp.where(place == 1, counts, 0.0))
    return jnp.concatenate([coded, tail], axis=0).astype(jnp.int32).astype(jnp.int16)


def unpack(coded, rows):
    wide = coded.astype(jnp.int32).astype(jnp.float32)
    scale = jnp.exp2(wide[rows : rows + 1] * (1.0 / STEPS)) * (1.0 / TOP)
    return wide[:rows] * scale, wide[rows + 1 : rows + 2]


def class_counts(metas, classes, lane_shape):
    lane = lax.broadcasted_iota(jnp.int32, lane_shape, 1)
    rows = [jnp.zeros(lane_shape, jnp.float32) for _ in range(classes)]
    for meta in metas:
        for p in range(meta.shape[1]):
            hit = lane == meta[1, p]
            for k in range(classes):
                rows[k] = rows[k] + jnp.where(hit & (meta[0, p] == k), 1.0, 0.0)
    return rows


def accumulate(metas, sources, tab, zz, total):
    total[...] = jnp.zeros_like(total)
    for meta, source in zip(metas, sources):

        def add(p, carry):
            k = meta[0, p]
            weight = tab[meta[1, p], zz]
            for c in range(CORES):
                total[k, c] += weight * source[p, c, zz].astype(jnp.float32)
            return carry

        lax.fori_loop(0, source.shape[0], add, 0)


def sum_first(n_cls, n_z, by_z, own_meta, got_meta, pos, own, got, tab, *rest):
    outs, total, count_rows = rest[:-2], rest[-2], rest[-1]
    metas, sources = (own_meta, got_meta), (own, got)
    classes = total.shape[0]
    held = classes // n_cls
    for k, row in enumerate(class_counts(metas, classes, (SUB, LANES))):
        count_rows[k] = row
    for j in range(n_z):
        zz = partner(pos[1], j, n_z)
        accumulate(metas, sources, tab, zz, total)
        if by_z:
            for k in range(classes):
                for c in range(2):
                    outs[j][k, c] = pack(total[k, c], count_rows[k, 0:1])
        else:
            for i in range(n_cls):
                to = partner(pos[0], i, n_cls)
                for h in range(held):
                    k = to * held + h
                    for c in range(2):
                        outs[c * n_cls + i][h, zz] = pack(total[k, c], count_rows[k, 0:1])


def join(parts, index, rows):
    value, counts = unpack(parts[0][index], rows)
    for part in parts[1:]:
        more, extra = unpack(part[index], rows)
        value, counts = value + more, counts + extra
    return value, counts


def sum_cls(n_cls, n_z, rows, pos, *refs):
    parts, outs = refs[:n_cls], refs[n_cls:]
    for j in range(n_z):
        zz = partner(pos[1], j, n_z)
        for h in range(parts[0].shape[0]):
            outs[j][h] = pack(*join(parts, (h, zz), rows))


def sum_z(n_cls, n_z, rows, pos, *refs):
    parts, outs = refs[:n_z], refs[n_z:]
    held = parts[0].shape[0] // n_cls
    for i in range(n_cls):
        to = partner(pos[0], i, n_cls)
        for h in range(held):
            for c in range(2):
                outs[i][h, c] = pack(*join(parts, (to * held + h, c), rows))


def finish(n_cls, n_z, rows_a, rows_b, pos, tab_a, tab_b, *refs):
    planes = [refs[c * n_z : (c + 1) * n_z] for c in range(2)]
    tail = refs[2 * n_z : 2 * n_z + n_cls]
    average, weights = refs[2 * n_z + n_cls :]
    lane = lax.broadcasted_iota(jnp.int32, (1, LANES), 1)
    for h in range(average.shape[0]):
        sums = [join(planes[c], (h,), rows_a) for c in range(2)]
        ends = [join(tail, (h, c), rows_b) for c in range(2)]
        counts = sums[0][1]
        weight_a = jnp.zeros((rows_a, LANES), jnp.float32)
        weight_b = jnp.zeros((rows_b, LANES), jnp.float32)
        for w in range(tab_a.shape[0]):
            number = jnp.sum(jnp.where(lane == w, counts, 0.0), axis=1, keepdims=True)
            weight_a = weight_a + number * (tab_a[w, pos[1]] * tab_a[w, pos[1]])
            weight_b = weight_b + number * (tab_b[w, pos[1]] * tab_b[w, pos[1]])
        weights[h, :rows_a] = weight_a
        weights[h, rows_a:] = weight_b
        for c in range(2):
            average[h, c, :rows_a] = sums[c][0] / (weight_a + 1.0)
            average[h, c, rows_a:] = ends[c][0] / (weight_b + 1.0)


def call(body, operands, shapes, scratch=(), smem=1, cost=1 << 20):
    return pl.pallas_call(
        body,
        out_shape=shapes,
        in_specs=[SMEM] * smem + [VMEM] * (len(operands) - smem),
        out_specs=[VMEM] * len(shapes),
        scratch_shapes=list(scratch),
        compiler_params=PARAMS,
        cost_estimate=pl.CostEstimate(flops=cost, bytes_accessed=cost, transcendentals=0),
    )(*operands)


def per_device(n_class, particles, labels, wedge_index, wedge_table):
    n_cls, n_dom = lax.axis_size("cls"), lax.axis_size("dom")
    n_z = n_dom // CORES
    p_dev, parts, voxels = particles.shape
    rows = voxels // (n_dom * LANES)
    held = n_class // n_cls
    dom = lax.axis_index("dom")
    core = lax.rem(dom, CORES)
    pos = jnp.stack([lax.axis_index("cls"), dom // CORES]).astype(jnp.int32)

    swap = [(d, d ^ 1) for d in range(n_dom)]
    z_moves = [
        [(d, int(partner_of(d // CORES, j, n_z)) * CORES + d % CORES) for d in range(n_dom)]
        for j in range(n_z)
    ]
    cls_moves = [[(d, int(partner_of(d, i, n_cls))) for d in range(n_cls)] for i in range(n_cls)]

    meta = jnp.stack([labels[:, 0], wedge_index])
    got_meta = lax.ppermute(meta, "dom", swap)

    rows_a = -(-(rows * 72 // 100) // SUB) * SUB - 2
    cuts = ((0, rows_a), (rows_a, rows))
    wide = particles.reshape(p_dev, parts, n_z, CORES, rows, LANES)
    table = wedge_table.reshape(-1, n_z, CORES, rows, LANES)
    own, got, tab = [], [], []
    for low, high in cuts:
        piece = wide[:, :, :, :, low:high]
        away = lax.dynamic_index_in_dim(piece, 1 - core, 3, keepdims=False)
        got.append(lax.ppermute(away, "dom", swap))
        own.append(lax.dynamic_index_in_dim(piece, core, 3, keepdims=False))
        tab.append(lax.dynamic_index_in_dim(table[:, :, :, low:high], core, 2, keepdims=False))

    rows_b = rows - rows_a
    size_a, size_b = padded(rows_a), padded(rows_b)

    def ints(*dims):
        return jax.ShapeDtypeStruct(dims + (LANES,), jnp.int16)

    def first(which, by_z, shapes):
        return call(
            functools.partial(sum_first, n_cls, n_z, by_z),
            (meta, got_meta, pos, own[which], got[which], tab[which]),
            shapes,
            scratch=(
                pltpu.VMEM((n_class, parts) + own[which].shape[-2:], jnp.float32),
                pltpu.VMEM((n_class, SUB, LANES), jnp.float32),
            ),
            smem=3,
        )

    head = first(0, False, [ints(held, n_z, size_a)] * (parts * n_cls))
    ends = first(1, True, [ints(n_class, parts, size_b)] * n_z)

    def over(axis, moves, arrays):
        return [arrays[0]] + [lax.ppermute(a, axis, m) for a, m in zip(arrays[1:], moves[1:])]

    moved = [over("cls", cls_moves, head[c * n_cls : (c + 1) * n_cls]) for c in range(parts)]
    ends = over("dom", z_moves, ends)
    planes = []
    for c in range(parts):
        coded = call(
            functools.partial(sum_cls, n_cls, n_z, rows_a),
            (pos, *moved[c]),
            [ints(held, size_a)] * n_z,
        )
        planes.extend(over("dom", z_moves, coded))
    coded = call(
        functools.partial(sum_z, n_cls, n_z, rows_b),
        (pos, *ends),
        [ints(held, parts, size_b)] * n_cls,
    )
    ends = over("cls", cls_moves, coded)
    average, weights = call(
        functools.partial(finish, n_cls, n_z, rows_a, rows_b),
        (pos, tab[0], tab[1], *planes, *ends),
        [
            jax.ShapeDtypeStruct((held, parts, rows, LANES), jnp.float32),
            jax.ShapeDtypeStruct((held, rows, LANES), jnp.float32),
        ],
    )
    return average.reshape(held, parts, -1), weights.reshape(held, -1)


def partner_of(index, offset, count):
    return index ^ offset if count & (count - 1) == 0 else (index + offset) % count


def solution(mesh):
    n_class = 2 * mesh.shape["cls"]
    return jax.shard_map(
        functools.partial(per_device, n_class),
        mesh=mesh,
        in_specs=(P(("cls", "dom"), None, None), P(("cls", "dom"), None), P(("cls", "dom")), P()),
        out_specs=(P("cls", None, "dom"), P("cls", "dom")),
        check_vma=False,
    )
```

time: 186 us -> 84.3 us (0.45)
  blocking collectives: 78.5 us -> 0 us
  waiting for transfers between devices: 55.5 us -> 12.1 us
  local copies, waits for them, and re-layouts: 11.2 us -> 34.2 us
  starting transfers between devices: 6.39 us -> 29.1 us
  between operations: 14.8 us -> 0.77 us
  other arithmetic: 11 us -> 0.08 us
  matrix products: 7.9 us -> 0 us
  Pallas kernels: 0 us -> 7.66 us
    unnamed x1 -> x0, blocking collectives: 78.5 us -> none
    unnamed x2 -> x0, waiting for transfers between devices: 55.5 us -> none
    ppermute x0 -> x21, starting transfers between devices: none -> 29.1 us  [the longest x18 28 us: over(): lax.ppermute(a, axis, m)]
    slice x0 -> x4, local copies, waits for them, and re-layouts: none -> 12.7 us  [the longest x2 7.29 us: per_device(): table[:, :, :, low:high]]
    ppermute x0 -> x21, waiting for transfers between devices: none -> 12.1 us  [the longest x18 12.1 us: over(): lax.ppermute(a, axis, m)]
    dot_general x3 -> x0, matrix products: 7.9 us -> none  [the longest x1 3.06 us: per_device(): jnp.einsum('kp,pcv->kcv', member, weighted, precision=lax.Precision.HIGHEST)]
    pallas_call x0 -> x6, Pallas kernels: none -> 7.66 us  [call(): pl.pallas_call(body, out_shape=shapes, in_specs=[SMEM] * smem + [VMEM] *...]
    mul x1 -> x0, other arithmetic: 6.44 us -> none  [per_device(): weighted = weight[:, None, :] * got_data]
  transfers between devices with their start and end apart: 2 -> 21, of which waited for: 1 -> 5; matrix products, arithmetic and copies ran while one was open for 5% -> 21% of each run, Pallas kernels for 0% -> 8%
where the time goes in v1:
time: 84.3 us; the launch traced here: 83.8 us
  local copies, waits for them, and re-layouts  34.2 us (41%)
  starting transfers between devices  29.1 us (35%)
  waiting for transfers between devices  12.1 us (14%)
  Pallas kernels  7.66 us (9%)
    ppermute x18, starting transfers between devices, over(): lax.ppermute(a, axis, m)  28 us
    ppermute x18, waiting for transfers between devices, over(): lax.ppermute(a, axis, m)  12.1 us
    pallas_call x6, Pallas kernels, call(): pl.pallas_call(body, out_shape=shapes, in_specs=[SMEM] * smem + [VMEM] *...  7.66 us
    reshape x1, local copies, waits for them, and re-layouts, per_device(): wide = particles.reshape(p_dev, parts, n_z, CORES, rows, LANES)  7.39 us
    slice x2, local copies, waits for them, and re-layouts, per_device(): table[:, :, :, low:high]  7.29 us
    slice x2, local copies, waits for them, and re-layouts, per_device(): piece = wide[:, :, :, :, low:high]  5.43 us
    reshape x1, local copies, waits for them, and re-layouts, per_device(): table = wedge_table.reshape(-1, n_z, CORES, rows, LANES)  5.26 us
    dynamic_slice x2, local copies, waits for them, and re-layouts, per_device(): away = lax.dynamic_index_in_dim(piece, 1 - core, 3, keepdims=False)  3.85 us
  transfers between devices with their start and end apart: 21, of which 5 were waited for; matrix products, arithmetic and copies ran while one was open for 21% of the time, Pallas kernels for 8%

profile of v1, /device:TPU:0, one launch (start us, length us, event | category | flops | bytes accessed | tf_op | source)
XLA Modules:
  0.0 83.8 jit_solution(4569868502215000086)
XLA Ops:
  0.6 7.4 %reshape.20 = bf16[8,2,4,2,108,128]{5,4,3,2,1,0:T(8,128)(2,1)} reshape(bf16[8,2,110592]{2,1,0:T(2,128)(2,1)} %param.4) | data formatting | bytes 7077888 | tf_op jit(solution)/shard_map/reshape | solution.py:185
  8.0 3.5 %slice.18 = bf16[8,2,4,2,78,128]{5,4,3,2,1,0:T(8,128)(2,1)} slice(bf16[8,2,4,2,108,128]{5,4,3,2,1,0:T(8,128)(2,1)} %reshape.20), slice={[0:8], [0:2], [0:4], [0:2], [0:78], [0:128]} | slice | bytes 5111808 | tf_op jit(solution)/shard_map/slice | solution.py:189
  11.6 2.0 %constant_dynamic-slice_fusion = (bf16[8,2,4,1,78,128]{5,4,3,2,1,0:T(8,128)(2,1)S(1)}, bf16[8,2,4,78,128]{4,3,2,1,0:T(8,128)(2,1)S(1)}) fusion(bf16[8,2,4,2,78,128]{5,4,3,2,1,0:T(8,128)(2,1)} %slice.18, s32[]{:T(128)S(6)} %select_n.21, s32[]{:T(128)S(6)} %select_n.20), kind=kLoop, calls=%fused_computation.7 | loop fusion | bytes 5111816 | tf_op jit(solution)/shard_map/jit(dynamic_index_in_dim)/dynamic_slice | solution.py:190
  13.5 1.9 %copy.40 = bf16[8,2,4,1,78,128]{5,0,4,3,2,1:T(8,128)(2,1)} copy(bf16[8,2,4,1,78,128]{5,4,3,2,1,0:T(8,128)(2,1)S(1)} %get-tuple-element.54) | data formatting | bytes 2555904 | tf_op jit(solution)/shard_map/jit(dynamic_index_in_dim)/dynamic_slice | solution.py:190
  15.9 1.9 %slice.19 = bf16[8,2,4,2,30,128]{5,4,3,2,1,0:T(8,128)(2,1)S(1)} slice(bf16[8,2,4,2,108,128]{5,4,3,2,1,0:T(8,128)(2,1)} %reshape.20), slice={[0:8], [0:2], [0:4], [0:2], [78:108], [0:128]} | slice | bytes 1966080 | tf_op jit(solution)/shard_map/slice | solution.py:189
  18.6 5.3 %reshape.16 = f32[12,4,2,108,128]{4,3,2,1,0:T(8,128)} reshape(f32[12,110592]{1,0:T(8,128)} %param.7) | data formatting | bytes 10616832 | tf_op jit(solution)/shard_map/reshape | solution.py:186
  23.9 4.3 %slice.16 = f32[12,4,2,78,128]{4,3,2,1,0:T(8,128)} slice(f32[12,4,2,108,128]{4,3,2,1,0:T(8,128)} %reshape.16), slice={[0:12], [0:4], [0:2], [0:78], [0:128]} | slice | bytes 7667712 | tf_op jit(solution)/shard_map/slice | solution.py:193
  28.2 3.0 %slice.17 = f32[12,4,2,30,128]{4,3,2,1,0:T(8,128)} slice(f32[12,4,2,108,128]{4,3,2,1,0:T(8,128)} %reshape.16), slice={[0:12], [0:4], [0:2], [78:108], [0:128]} | slice | bytes 2949120 | tf_op jit(solution)/shard_map/slice | solution.py:193
  31.2 1.7 %dynamic-slice_bitcast_fusion.tab.tab_a = f32[12,4,78,128]{3,2,1,0:T(8,128)S(1)} fusion(f32[12,4,2,78,128]{4,3,2,1,0:T(8,128)} %slice.16, s32[]{:T(128)S(6)} %select_n.20), kind=kLoop, calls=%fused_computation | loop fusion | bytes 3833860 | tf_op jit(solution)/shard_map/jit(dynamic_index_in_dim)/squeeze | solution.py:193
  32.9 1.6 %copy.23.got = bf16[8,2,4,78,128]{4,3,2,1,0:T(8,128)(2,1)S(1)} copy(bf16[8,2,4,78,128]{4,0,3,2,1:T(8,128)(2,1)} %collective-permute-done.1) | data formatting | bytes 2555904 | tf_op jit(solution)/shard_map/ppermute | solution.py:191
  34.5 2.5 %shard_map.59 = (s16[2,4,80,128]{3,2,1,0:T(8,128)(2,1)S(1)}, s16[2,4,80,128]{3,2,1,0:T(8,128)(2,1)S(1)}, s16[2,4,80,128]{3,2,1,0:T(8,128)(2,1)S(1)}, s16[2,4,80,...) custom-call(s32[2,8]{1,0:T(2,128)S(1)} %pad_add_fusion.own_meta, ...), custom_call_target="tpu_custom_call" | custom-call | flops 1048576 | bytes 1048576 | tf_op jit(solution)/shard_map/pallas_call | solution.py:152
  37.0 2.6 %collective-permute-start.2 = (s16[2,4,80,128]{3,2,1,0:T(8,128)(2,1)S(1)}, s16[2,4,80,128]{3,2,1,0:T(8,128)(2,1)S(1)}, u32[]{:S(2)}, u32[]{:S(2)}) collective-permute-start(s16[2,4,80,128]{3,2,1,0:T(8,128)(2,1)S(1)} %get-tuple-element.29), channel_id=1, source_target_pairs={{0,8},{8,0},{16,24},{24,16},{1,9},{9,1},{17,25},{25,17},{2,10},{10... | collective-permute-start | bytes 491528 | tf_op jit(solution)/shard_map/ppermute | solution.py:217
  39.6 1.5 %collective-permute-start.3 = (s16[2,4,80,128]{3,2,1,0:T(8,128)(2,1)S(1)}, s16[2,4,80,128]{3,2,1,0:T(8,128)(2,1)S(1)}, u32[]{:S(2)}, u32[]{:S(2)}) collective-permute-start(s16[2,4,80,128]{3,2,1,0:T(8,128)(2,1)S(1)} %get-tuple-element.30), channel_id=1, source_target_pairs={{0,16},{8,24},{16,0},{24,8},{1,17},{9,25},{17,1},{25,9},{2,18},{10... | collective-permute-start | bytes 491528 | tf_op jit(solution)/shard_map/ppermute | solution.py:217
  41.2 1.9 %shard_map.62 = (s16[8,2,32,128]{3,2,1,0:T(8,128)(2,1)S(1)}, s16[8,2,32,128]{3,2,1,0:T(8,128)(2,1)S(1)}, s16[8,2,32,128]{3,2,1,0:T(8,128)(2,1)S(1)}, s16[8,2,32,128]{3,2,1,0:T(8,128)(2,1)S(1)}) custom-call(s32[2,8]{1,0:T(2,128)S(1)} %pad_add_fusion.own_meta, s32[2,8]{1,0:T(2,128)S(1)} %collective-permute-done.got_meta, s32[2]{0:T(128)S(1)} %pad_add_fusion.1.pos, ...), custom_call_target="tpu_custom_call" | custom-call | flops 1048576 | bytes 1048576 | tf_op jit(solution)/shard_map/pallas_call | solution.py:152
  43.0 2.1 %collective-permute-start.15 = (s16[8,2,32,128]{3,2,1,0:T(8,128)(2,1)S(1)}, s16[8,2,32,128]{3,2,1,0:T(8,128)(2,1)S(1)}, u32[]{:S(2)}, u32[]{:S(2)}) collective-permute-start(s16[8,2,32,128]{3,2,1,0:T(8,128)(2,1)S(1)} %get-tuple-element.45), channel_id=1, source_target_pairs={{0,2},{1,3},{2,0},{3,1},{4,6},{5,7},{6,4},{7,5},{8,10},{9,11},{10,... | collective-permute-start | bytes 393224 | tf_op jit(solution)/shard_map/ppermute | solution.py:217
  45.1 1.5 %collective-permute-start.8 = (s16[2,4,80,128]{3,2,1,0:T(8,128)(2,1)S(1)}, s16[2,4,80,128]{3,2,1,0:T(8,128)(2,1)S(1)}, u32[]{:S(2)}, u32[]{:S(2)}) collective-permute-start(s16[2,4,80,128]{3,2,1,0:T(8,128)(2,1)S(1)} %get-tuple-element.37), channel_id=1, source_target_pairs={{0,8},{8,0},{16,24},{24,16},{1,9},{9,1},{17,25},{25,17},{2,10},{10... | collective-permute-start | bytes 491528 | tf_op jit(solution)/shard_map/ppermute | solution.py:217
  46.6 1.8 %collective-permute-done.15.refs_1_ = s16[8,2,32,128]{3,2,1,0:T(8,128)(2,1)S(1)} collective-permute-done((s16[8,2,32,128]{3,2,1,0:T(8,128)(2,1)S(1)}, s16[8,2,32,128]{3,2,1,0:T(8,128)(2,1)S(1)}, u32[]{:S(2)}, u32[]{:S(2)}) %collective-permute-start.15) | collective-permute-done | bytes 131104 | tf_op jit(solution)/shard_map/ppermute | solution.py:217
  48.4 1.7 %collective-permute-start.9 = (s16[2,4,80,128]{3,2,1,0:T(8,128)(2,1)S(1)}, s16[2,4,80,128]{3,2,1,0:T(8,128)(2,1)S(1)}, u32[]{:S(2)}, u32[]{:S(2)}) collective-permute-start(s16[2,4,80,128]{3,2,1,0:T(8,128)(2,1)S(1)} %get-tuple-element.38), channel_id=1, source_target_pairs={{0,16},{8,24},{16,0},{24,8},{1,17},{9,25},{17,1},{25,9},{2,18},{10... | collective-permute-start | bytes 491528 | tf_op jit(solution)/shard_map/ppermute | solution.py:217
  50.1 2.6 %collective-permute-start.16 = (s16[8,2,32,128]{3,2,1,0:T(8,128)(2,1)S(1)}, s16[8,2,32,128]{3,2,1,0:T(8,128)(2,1)S(1)}, u32[]{:S(2)}, u32[]{:S(2)}) collective-permute-start(s16[8,2,32,128]{3,2,1,0:T(8,128)(2,1)S(1)} %get-tuple-element.46), channel_id=1, source_target_pairs={{0,4},{1,5},{2,6},{3,7},{4,0},{5,1},{6,2},{7,3},{8,12},{9,13},{10,... | collective-permute-start | bytes 393224 | tf_op jit(solution)/shard_map/ppermute | solution.py:217
  52.7 1.4 %collective-permute-start.10 = (s16[2,4,80,128]{3,2,1,0:T(8,128)(2,1)S(1)}, s16[2,4,80,128]{3,2,1,0:T(8,128)(2,1)S(1)}, u32[]{:S(2)}, u32[]{:S(2)}) collective-permute-start(s16[2,4,80,128]{3,2,1,0:T(8,128)(2,1)S(1)} %get-tuple-element.39), channel_id=1, source_target_pairs={{0,24},{8,16},{16,8},{24,0},{1,25},{9,17},{17,9},{25,1},{2,26},{10... | collective-permute-start | bytes 491528 | tf_op jit(solution)/shard_map/ppermute | solution.py:217
  54.2 1.4 %collective-permute-start.17 = (s16[8,2,32,128]{3,2,1,0:T(8,128)(2,1)S(1)}, s16[8,2,32,128]{3,2,1,0:T(8,128)(2,1)S(1)}, u32[]{:S(2)}, u32[]{:S(2)}) collective-permute-start(s16[8,2,32,128]{3,2,1,0:T(8,128)(2,1)S(1)} %get-tuple-element.47), channel_id=1, source_target_pairs={{0,6},{1,7},{2,4},{3,5},{4,2},{5,3},{6,0},{7,1},{8,14},{9,15},{10,... | collective-permute-start | bytes 393224 | tf_op jit(solution)/shard_map/ppermute | solution.py:217
  55.5 0.8 shard_map.60
  56.3 4.9 %collective-permute-done.16.refs_2_ = s16[8,2,32,128]{3,2,1,0:T(8,128)(2,1)S(1)} collective-permute-done((s16[8,2,32,128]{3,2,1,0:T(8,128)(2,1)S(1)}, s16[8,2,32,128]{3,2,1,0:T(8,128)(2,1)S(1)}, u32[]{:S(2)}, u32[]{:S(2)}) %collective-permute-start.16) | collective-permute-done | bytes 131104 | tf_op jit(solution)/shard_map/ppermute | solution.py:217
  61.2 0.9 %collective-permute-start.5 = (s16[2,80,128]{2,1,0:T(8,128)(2,1)S(1)}, s16[2,80,128]{2,1,0:T(8,128)(2,1)S(1)}, u32[]{:S(2)}, u32[]{:S(2)}) collective-permute-start(s16[2,80,128]{2,1,0:T(8,128)(2,1)S(1)} %get-tuple-element.33), channel_id=1, source_target_pairs={{0,2},{1,3},{2,0},{3,1},{4,6},{5,7},{6,4},{7,5},{8,10},{9,11},{10,... | collective-permute-start | bytes 122888 | tf_op jit(solution)/shard_map/ppermute | solution.py:217
  63.0 1.6 %collective-permute-start.18 = (s16[2,2,32,128]{3,2,1,0:T(8,128)(2,1)S(1)}, s16[2,2,32,128]{3,2,1,0:T(8,128)(2,1)S(1)}, u32[]{:S(2)}, u32[]{:S(2)}) collective-permute-start(s16[2,2,32,128]{3,2,1,0:T(8,128)(2,1)S(1)} %get-tuple-element.49), channel_id=1, source_target_pairs={{0,8},{8,0},{16,24},{24,16},{1,9},{9,1},{17,25},{25,17},{2,10},{10... | collective-permute-start | bytes 98312 | tf_op jit(solution)/shard_map/ppermute | solution.py:217
  65.1 1.4 %collective-permute-start.20 = (s16[2,2,32,128]{3,2,1,0:T(8,128)(2,1)S(1)}, s16[2,2,32,128]{3,2,1,0:T(8,128)(2,1)S(1)}, u32[]{:S(2)}, u32[]{:S(2)}) collective-permute-start(s16[2,2,32,128]{3,2,1,0:T(8,128)(2,1)S(1)} %get-tuple-element.51), channel_id=1, source_target_pairs={{0,24},{8,16},{16,8},{24,0},{1,25},{9,17},{17,9},{25,1},{2,26},{10... | collective-permute-start | bytes 98312 | tf_op jit(solution)/shard_map/ppermute | solution.py:217
  66.5 3.8 %collective-permute-start.6 = (s16[2,80,128]{2,1,0:T(8,128)(2,1)S(1)}, s16[2,80,128]{2,1,0:T(8,128)(2,1)S(1)}, u32[]{:S(2)}, u32[]{:S(2)}) collective-permute-start(s16[2,80,128]{2,1,0:T(8,128)(2,1)S(1)} %get-tuple-element.34), channel_id=1, source_target_pairs={{0,4},{1,5},{2,6},{3,7},{4,0},{5,1},{6,2},{7,3},{8,12},{9,13},{10,... | collective-permute-start | bytes 122888 | tf_op jit(solution)/shard_map/ppermute | solution.py:217
  71.8 3.8 %collective-permute-start.12 = (s16[2,80,128]{2,1,0:T(8,128)(2,1)S(1)}, s16[2,80,128]{2,1,0:T(8,128)(2,1)S(1)}, u32[]{:S(2)}, u32[]{:S(2)}) collective-permute-start(s16[2,80,128]{2,1,0:T(8,128)(2,1)S(1)} %get-tuple-element.42), channel_id=1, source_target_pairs={{0,4},{1,5},{2,6},{3,7},{4,0},{5,1},{6,2},{7,3},{8,12},{9,13},{10,... | collective-permute-start | bytes 122888 | tf_op jit(solution)/shard_map/ppermute | solution.py:217
  76.1 1.0 %collective-permute-done.7.refs_3_ = s16[2,80,128]{2,1,0:T(8,128)(2,1)S(1)} collective-permute-done((s16[2,80,128]{2,1,0:T(8,128)(2,1)S(1)}, s16[2,80,128]{2,1,0:T(8,128)(2,1)S(1)}, u32[]{:S(2)}, u32[]{:S(2)}) %collective-permute-start.7) | collective-permute-done | bytes 40992 | tf_op jit(solution)/shard_map/ppermute | solution.py:217
  77.0 1.4 %collective-permute-done.12.refs_6_ = s16[2,80,128]{2,1,0:T(8,128)(2,1)S(1)} collective-permute-done((s16[2,80,128]{2,1,0:T(8,128)(2,1)S(1)}, s16[2,80,128]{2,1,0:T(8,128)(2,1)S(1)}, u32[]{:S(2)}, u32[]{:S(2)}) %collective-permute-start.12) | collective-permute-done | bytes 40992 | tf_op jit(solution)/shard_map/ppermute | solution.py:217
  78.5 2.9 %collective-permute-done.13.refs_7_ = s16[2,80,128]{2,1,0:T(8,128)(2,1)S(1)} collective-permute-done((s16[2,80,128]{2,1,0:T(8,128)(2,1)S(1)}, s16[2,80,128]{2,1,0:T(8,128)(2,1)S(1)}, u32[]{:S(2)}, u32[]{:S(2)}) %collective-permute-start.13) | collective-permute-done | bytes 40992 | tf_op jit(solution)/shard_map/ppermute | solution.py:217
  81.4 0.9 %shard_map.64 = (f32[2,2,108,128]{3,2,1,0:T(8,128)S(1)}, f32[2,108,128]{2,1,0:T(8,128)S(1)}) custom-call(s32[2]{0:T(128)S(1)} %pad_add_fusion.1.pos, f32[12,4,78,128]{3,2,1,0:T(8,128)S(1)} %dynamic-slice_bitcast_fusion.tab.tab_a, f32[12,4,30,128]{3,2,1,0:T(8,128)S(1)} %dynamic-slice_bitcast_fusion.2.tab.tab_b, ...), custom_call_target="tpu_custom_call" | custom-call | flops 1048576 | bytes 1048576 | tf_op jit(solution)/shard_map/pallas_call | solution.py:152
  (38 shorter events, 6.2 us)
Async XLA Ops:
  15.4 2.6 %copy-start.1 = (s32[8]{0:T(128)S(1)}, s32[8]{0:T(128)}, u32[]{:S(2)}) copy-start(s32[8]{0:T(128)} %param.6) | copy-start | bytes 100
  15.4 2.6 %copy-start.2 = (s32[8,1]{0,1:T(1,128)S(1)}, s32[8,1]{0,1:T(1,128)}, u32[]{:S(2)}) copy-start(s32[8,1]{0,1:T(1,128)} %param.5) | copy-start | bytes 100
  15.4 17.5 %collective-permute-start.1 = (bf16[8,2,4,78,128]{4,0,3,2,1:T(8,128)(2,1)}, bf16[8,2,4,78,128]{4,0,3,2,1:T(8,128)(2,1)}, u32[]{:S(2)}, u32[]{:S(2)}) collective-permute-start(bf16[8,2,4,78,128]{4,0,3,2,1:T(8,128)(2,1)} %bitcast.25), channel_id=1, source_target_pairs={{0,1},{1,0},{2,3},{3,2},{4,5},{5,4},{6,7},{7,6},{8,9},{9,8},{10,11... | collective-permute-start | bytes 3833864 | tf_op jit(solution)/shard_map/ppermute | solution.py:191
  17.9 23.2 %collective-permute-start.14 = (bf16[8,2,4,30,128]{4,3,2,1,0:T(8,128)(2,1)S(1)}, bf16[8,2,4,30,128]{4,3,2,1,0:T(8,128)(2,1)S(1)}, u32[]{:S(2)}, u32[]{:S(2)}) collective-permute-start(bf16[8,2,4,30,128]{4,3,2,1,0:T(8,128)(2,1)S(1)} %get-tuple-element.56), channel_id=1, source_target_pairs={{0,1},{1,0},{2,3},{3,2},{4,5},{5,4},{6,7},{7,6},{8,9},{9,8},{10,11... | collective-permute-start | bytes 1474568 | tf_op jit(solution)/shard_map/ppermute | solution.py:191
  18.1 16.4 %collective-permute-start = (s32[2,8]{1,0:T(2,128)S(1)}, s32[2,8]{1,0:T(2,128)S(1)}, u32[]{:S(2)}, u32[]{:S(2)}) collective-permute-start(s32[2,8]{1,0:T(2,128)S(1)} %pad_add_fusion.own_meta), channel_id=1, source_target_pairs={{0,1},{1,0},{2,3},{3,2},{4,5},{5,4},{6,7},{7,6},{8,9},{9,8},{10,11... | collective-permute-start | bytes 200 | tf_op jit(solution)/shard_map/ppermute | solution.py:181
  34.5 6.6 %copy-start = (f32[12,4,2,30,128]{4,3,2,1,0:T(8,128)S(1)}, f32[12,4,2,30,128]{4,3,2,1,0:T(8,128)}, u32[]{:S(2)}) copy-start(f32[12,4,2,30,128]{4,3,2,1,0:T(8,128)} %slice.17) | copy-start | bytes 4423684
  37.0 13.1 %collective-permute-start.2 = (s16[2,4,80,128]{3,2,1,0:T(8,128)(2,1)S(1)}, s16[2,4,80,128]{3,2,1,0:T(8,128)(2,1)S(1)}, u32[]{:S(2)}, u32[]{:S(2)}) collective-permute-start(s16[2,4,80,128]{3,2,1,0:T(8,128)(2,1)S(1)} %get-tuple-element.29), channel_id=1, source_target_pairs={{0,8},{8,0},{16,24},{24,16},{1,9},{9,1},{17,25},{25,17},{2,10},{10... | collective-permute-start | bytes 491528 | tf_op jit(solution)/shard_map/ppermute | solution.py:217
  39.6 13.1 %collective-permute-start.3 = (s16[2,4,80,128]{3,2,1,0:T(8,128)(2,1)S(1)}, s16[2,4,80,128]{3,2,1,0:T(8,128)(2,1)S(1)}, u32[]{:S(2)}, u32[]{:S(2)}) collective-permute-start(s16[2,4,80,128]{3,2,1,0:T(8,128)(2,1)S(1)} %get-tuple-element.30), channel_id=1, source_target_pairs={{0,16},{8,24},{16,0},{24,8},{1,17},{9,25},{17,1},{25,9},{2,18},{10... | collective-permute-start | bytes 491528 | tf_op jit(solution)/shard_map/ppermute | solution.py:217
  41.1 13.1 %collective-permute-start.4 = (s16[2,4,80,128]{3,2,1,0:T(8,128)(2,1)S(1)}, s16[2,4,80,128]{3,2,1,0:T(8,128)(2,1)S(1)}, u32[]{:S(2)}, u32[]{:S(2)}) collective-permute-start(s16[2,4,80,128]{3,2,1,0:T(8,128)(2,1)S(1)} %get-tuple-element.31), channel_id=1, source_target_pairs={{0,24},{8,16},{16,8},{24,0},{1,25},{9,17},{17,9},{25,1},{2,26},{10... | collective-permute-start | bytes 491528 | tf_op jit(solution)/shard_map/ppermute | solution.py:217
  43.0 5.4 %collective-permute-start.15 = (s16[8,2,32,128]{3,2,1,0:T(8,128)(2,1)S(1)}, s16[8,2,32,128]{3,2,1,0:T(8,128)(2,1)S(1)}, u32[]{:S(2)}, u32[]{:S(2)}) collective-permute-start(s16[8,2,32,128]{3,2,1,0:T(8,128)(2,1)S(1)} %get-tuple-element.45), channel_id=1, source_target_pairs={{0,2},{1,3},{2,0},{3,1},{4,6},{5,7},{6,4},{7,5},{8,10},{9,11},{10,... | collective-permute-start | bytes 393224 | tf_op jit(solution)/shard_map/ppermute | solution.py:217
  45.1 19.4 %collective-permute-start.8 = (s16[2,4,80,128]{3,2,1,0:T(8,128)(2,1)S(1)}, s16[2,4,80,128]{3,2,1,0:T(8,128)(2,1)S(1)}, u32[]{:S(2)}, u32[]{:S(2)}) collective-permute-start(s16[2,4,80,128]{3,2,1,0:T(8,128)(2,1)S(1)} %get-tuple-element.37), channel_id=1, source_target_pairs={{0,8},{8,0},{16,24},{24,16},{1,9},{9,1},{17,25},{25,17},{2,10},{10... | collective-permute-start | bytes 491528 | tf_op jit(solution)/shard_map/ppermute | solution.py:217
  48.4 16.7 %collective-permute-start.9 = (s16[2,4,80,128]{3,2,1,0:T(8,128)(2,1)S(1)}, s16[2,4,80,128]{3,2,1,0:T(8,128)(2,1)S(1)}, u32[]{:S(2)}, u32[]{:S(2)}) collective-permute-start(s16[2,4,80,128]{3,2,1,0:T(8,128)(2,1)S(1)} %get-tuple-element.38), channel_id=1, source_target_pairs={{0,16},{8,24},{16,0},{24,8},{1,17},{9,25},{17,1},{25,9},{2,18},{10... | collective-permute-start | bytes 491528 | tf_op jit(solution)/shard_map/ppermute | solution.py:217
  50.1 11.1 %collective-permute-start.16 = (s16[8,2,32,128]{3,2,1,0:T(8,128)(2,1)S(1)}, s16[8,2,32,128]{3,2,1,0:T(8,128)(2,1)S(1)}, u32[]{:S(2)}, u32[]{:S(2)}) collective-permute-start(s16[8,2,32,128]{3,2,1,0:T(8,128)(2,1)S(1)} %get-tuple-element.46), channel_id=1, source_target_pairs={{0,4},{1,5},{2,6},{3,7},{4,0},{5,1},{6,2},{7,3},{8,12},{9,13},{10,... | collective-permute-start | bytes 393224 | tf_op jit(solution)/shard_map/ppermute | solution.py:217
  52.7 13.8 %collective-permute-start.10 = (s16[2,4,80,128]{3,2,1,0:T(8,128)(2,1)S(1)}, s16[2,4,80,128]{3,2,1,0:T(8,128)(2,1)S(1)}, u32[]{:S(2)}, u32[]{:S(2)}) collective-permute-start(s16[2,4,80,128]{3,2,1,0:T(8,128)(2,1)S(1)} %get-tuple-element.39), channel_id=1, source_target_pairs={{0,24},{8,16},{16,8},{24,0},{1,25},{9,17},{17,9},{25,1},{2,26},{10... | collective-permute-start | bytes 491528 | tf_op jit(solution)/shard_map/ppermute | solution.py:217
  54.2 8.0 %collective-permute-start.17 = (s16[8,2,32,128]{3,2,1,0:T(8,128)(2,1)S(1)}, s16[8,2,32,128]{3,2,1,0:T(8,128)(2,1)S(1)}, u32[]{:S(2)}, u32[]{:S(2)}) collective-permute-start(s16[8,2,32,128]{3,2,1,0:T(8,128)(2,1)S(1)} %get-tuple-element.47), channel_id=1, source_target_pairs={{0,6},{1,7},{2,4},{3,5},{4,2},{5,3},{6,0},{7,1},{8,14},{9,15},{10,... | collective-permute-start | bytes 393224 | tf_op jit(solution)/shard_map/ppermute | solution.py:217
  61.2 14.4 %collective-permute-start.5 = (s16[2,80,128]{2,1,0:T(8,128)(2,1)S(1)}, s16[2,80,128]{2,1,0:T(8,128)(2,1)S(1)}, u32[]{:S(2)}, u32[]{:S(2)}) collective-permute-start(s16[2,80,128]{2,1,0:T(8,128)(2,1)S(1)} %get-tuple-element.33), channel_id=1, source_target_pairs={{0,2},{1,3},{2,0},{3,1},{4,6},{5,7},{6,4},{7,5},{8,10},{9,11},{10,... | collective-permute-start | bytes 122888 | tf_op jit(solution)/shard_map/ppermute | solution.py:217
  63.0 8.2 %collective-permute-start.18 = (s16[2,2,32,128]{3,2,1,0:T(8,128)(2,1)S(1)}, s16[2,2,32,128]{3,2,1,0:T(8,128)(2,1)S(1)}, u32[]{:S(2)}, u32[]{:S(2)}) collective-permute-start(s16[2,2,32,128]{3,2,1,0:T(8,128)(2,1)S(1)} %get-tuple-element.49), channel_id=1, source_target_pairs={{0,8},{8,0},{16,24},{24,16},{1,9},{9,1},{17,25},{25,17},{2,10},{10... | collective-permute-start | bytes 98312 | tf_op jit(solution)/shard_map/ppermute | solution.py:217
  64.6 7.1 %collective-permute-start.19 = (s16[2,2,32,128]{3,2,1,0:T(8,128)(2,1)S(1)}, s16[2,2,32,128]{3,2,1,0:T(8,128)(2,1)S(1)}, u32[]{:S(2)}, u32[]{:S(2)}) collective-permute-start(s16[2,2,32,128]{3,2,1,0:T(8,128)(2,1)S(1)} %get-tuple-element.50), channel_id=1, source_target_pairs={{0,16},{8,24},{16,0},{24,8},{1,17},{9,25},{17,1},{25,9},{2,18},{10... | collective-permute-start | bytes 98312 | tf_op jit(solution)/shard_map/ppermute | solution.py:217
  65.1 6.7 %collective-permute-start.20 = (s16[2,2,32,128]{3,2,1,0:T(8,128)(2,1)S(1)}, s16[2,2,32,128]{3,2,1,0:T(8,128)(2,1)S(1)}, u32[]{:S(2)}, u32[]{:S(2)}) collective-permute-start(s16[2,2,32,128]{3,2,1,0:T(8,128)(2,1)S(1)} %get-tuple-element.51), channel_id=1, source_target_pairs={{0,24},{8,16},{16,8},{24,0},{1,25},{9,17},{17,9},{25,1},{2,26},{10... | collective-permute-start | bytes 98312 | tf_op jit(solution)/shard_map/ppermute | solution.py:217
  66.5 9.5 %collective-permute-start.6 = (s16[2,80,128]{2,1,0:T(8,128)(2,1)S(1)}, s16[2,80,128]{2,1,0:T(8,128)(2,1)S(1)}, u32[]{:S(2)}, u32[]{:S(2)}) collective-permute-start(s16[2,80,128]{2,1,0:T(8,128)(2,1)S(1)} %get-tuple-element.34), channel_id=1, source_target_pairs={{0,4},{1,5},{2,6},{3,7},{4,0},{5,1},{6,2},{7,3},{8,12},{9,13},{10,... | collective-permute-start | bytes 122888 | tf_op jit(solution)/shard_map/ppermute | solution.py:217
  71.2 5.9 %collective-permute-start.7 = (s16[2,80,128]{2,1,0:T(8,128)(2,1)S(1)}, s16[2,80,128]{2,1,0:T(8,128)(2,1)S(1)}, u32[]{:S(2)}, u32[]{:S(2)}) collective-permute-start(s16[2,80,128]{2,1,0:T(8,128)(2,1)S(1)} %get-tuple-element.35), channel_id=1, source_target_pairs={{0,6},{1,7},{2,4},{3,5},{4,2},{5,3},{6,0},{7,1},{8,14},{9,15},{10,... | collective-permute-start | bytes 122888 | tf_op jit(solution)/shard_map/ppermute | solution.py:217
  71.7 5.4 %collective-permute-start.11 = (s16[2,80,128]{2,1,0:T(8,128)(2,1)S(1)}, s16[2,80,128]{2,1,0:T(8,128)(2,1)S(1)}, u32[]{:S(2)}, u32[]{:S(2)}) collective-permute-start(s16[2,80,128]{2,1,0:T(8,128)(2,1)S(1)} %get-tuple-element.41), channel_id=1, source_target_pairs={{0,2},{1,3},{2,0},{3,1},{4,6},{5,7},{6,4},{7,5},{8,10},{9,11},{10,... | collective-permute-start | bytes 122888 | tf_op jit(solution)/shard_map/ppermute | solution.py:217
  71.8 6.7 %collective-permute-start.12 = (s16[2,80,128]{2,1,0:T(8,128)(2,1)S(1)}, s16[2,80,128]{2,1,0:T(8,128)(2,1)S(1)}, u32[]{:S(2)}, u32[]{:S(2)}) collective-permute-start(s16[2,80,128]{2,1,0:T(8,128)(2,1)S(1)} %get-tuple-element.42), channel_id=1, source_target_pairs={{0,4},{1,5},{2,6},{3,7},{4,0},{5,1},{6,2},{7,3},{8,12},{9,13},{10,... | collective-permute-start | bytes 122888 | tf_op jit(solution)/shard_map/ppermute | solution.py:217
  75.6 5.8 %collective-permute-start.13 = (s16[2,80,128]{2,1,0:T(8,128)(2,1)S(1)}, s16[2,80,128]{2,1,0:T(8,128)(2,1)S(1)}, u32[]{:S(2)}, u32[]{:S(2)}) collective-permute-start(s16[2,80,128]{2,1,0:T(8,128)(2,1)S(1)} %get-tuple-element.43), channel_id=1, source_target_pairs={{0,6},{1,7},{2,4},{3,5},{4,2},{5,3},{6,0},{7,1},{8,14},{9,15},{10,... | collective-permute-start | bytes 122888 | tf_op jit(solution)/shard_map/ppermute | solution.py:217
